TPU v7x, 32 devices: a whole 2x2x4 slice. The times are simulated.
32 devices in a mesh: state: 2 (over x), bond: 16 (over z, y, core).
Axes of the slice: x: 2, y: 2, z: 4, core: 2. Of those that a mesh axis runs over, the one named last changes fastest.
Arguments:
- intersect_left: bfloat16 [2, 2048, 2048], P('state', 'bond'), may hold values from -0.125 to 0.125
- stored_block: bfloat16 [2, 4, 2048, 2048], P('state', None, 'bond'), may hold values from -6 to 6
- stored_site: bfloat16 [2, 2, 2048, 2048], P('state', None, 'bond'), may hold values from -6 to 6
- current_site: bfloat16 [2048, 2, 2048], P('bond', None, 'state'), may hold values from -0.09375 to 0.09375
- current_block: bfloat16 [4, 2048, 2048], P(None, 'bond', 'state'), may hold values from -6 to 6
- penalty_weight: float32 [2], replicated, may hold values from 0.5 to 4
Outputs:
- penalized: float32 [4, 2048, 2048], P(None, 'bond', 'state')
- intersect_next: bfloat16 [2, 2048, 2048], P('state', 'bond')
All inputs are finite; a program needn't handle non-finite values.
Results may differ from a plain program's by a relative error of at most 0.0055.
Values may be sent and summed in bfloat16 or wider, within the bound.
A program may use at most 64 MiB of HBM per device.

v0:
```python
import jax
import jax.numpy as jnp
from jax import lax
from jax.sharding import PartitionSpec as P


def contract_last(left, right):
    return lax.dot_general(
        left, right, (((1,), (1,)), ((), ())), preferred_element_type=jnp.float32
    )


def shards(intersect_left, stored_block, stored_site, current_site, current_block, penalty_weight):
    bond_width = intersect_left.shape[2]
    column_count = stored_block.shape[2]
    pair_count = stored_block.shape[1]
    physical = stored_site.shape[1]
    operand = jnp.concatenate(
        [
            stored_block[0].reshape(pair_count * column_count, bond_width),
            stored_site[0].reshape(physical * column_count, bond_width),
        ],
        axis=0,
    )
    products = contract_last(operand, lax.all_gather(intersect_left, "bond", axis=1, tiled=True)[0])
    projected = products[: pair_count * column_count].reshape(pair_count, column_count, bond_width)
    moved = (
        products[pair_count * column_count :]
        .astype(jnp.bfloat16)
        .reshape(1, physical, column_count, bond_width)
    )
    scale_factor = 1.0 / (physical * bond_width)
    whole_block = lax.all_gather(current_block, "state", axis=2, tiled=True)
    intersect = (
        lax.psum(jnp.sum(projected * whole_block.astype(jnp.float32)), "bond") * scale_factor
    )
    weight = penalty_weight[lax.axis_index("state")]
    summed = lax.psum_scatter(
        weight * intersect * projected, "state", scatter_dimension=2, tiled=True
    )
    penalized = current_block.astype(jnp.float32) + summed
    moved_all = lax.all_gather(moved, "state", axis=0, tiled=True)
    grown = jnp.einsum(
        "asf,ksea->kfe",
        lax.all_gather(current_site, "bond", axis=0, tiled=True),
        moved_all,
        preferred_element_type=jnp.float32,
    )
    intersect_next = lax.all_to_all(
        lax.all_to_all(
            grown.astype(jnp.bfloat16), "state", split_axis=0, concat_axis=1, tiled=True
        ),
        "bond",
        split_axis=1,
        concat_axis=2,
        tiled=True,
    )
    return (penalized, intersect_next)


def solution(mesh):
    placed = (
        P("state", "bond", None),
        P("state", None, "bond", None),
        P("state", None, "bond", None),
        P("bond", None, "state"),
        P(None, "bond", "state"),
        P(),
    )
    return jax.shard_map(
        shards,
        mesh=mesh,
        in_specs=placed,
        out_specs=(P(None, "bond", "state"), P("state", "bond", None)),
        check_vma=False,
    )
```

profile of v0, /device:TPU:27, one launch (start us, length us, event | category | flops | bytes accessed | tf_op | source)
XLA Modules:
  0.0 303.1 jit_solution(15348684443080593336)
XLA Ops:
  7.2 0.7 all-gather.5.cloned.1.call-update
  7.9 0.7 all-gather.7.cloned.1.call-update
  8.7 2.0 copy.15
  10.7 73.7 %all-gather.5.cloned.1.call-done = bf16[1,2048,2048]{2,1,0:T(8,128)(2,1)} async-done(((bf16[1,128,2048]{2,1,0:T(8,128)(2,1)}), bf16[1,2048,2048]{2,1,0:T(8,128)(2,1)}) %all-gather.5.cloned.1.call-update) | async-done | bytes 8388624 | tf_op jit(solution)/shard_map/all_gather | solution.py:25
  84.4 10.1 %fusion.2 = f32[768,2048]{1,0:T(8,128)S(1)} fusion(bf16[1,2048,2048]{2,1,0:T(8,128)(2,1)} %all-gather.5.cloned.1.call-done, bf16[256,2048]{1,0:T(8,128)(2,1)} %bitcast.45, bf16[512,2048]{1,0:T(8,128)(2,1)} %bitcast.44), kind=kOutput, calls=%fused_computation.2 | convolution fusion | flops 6448742400 | bytes 17825792 | tf_op jit(solution)/shard_map/dot_general | solution.py:8
  94.5 2.7 copy-done
  97.2 1.1 slice.13
  98.4 4.7 %slice.9 = f32[512,2048]{1,0:T(8,128)} slice(f32[768,2048]{1,0:T(8,128)} %copy-done), slice={[0:512], [0:2048]} | slice | bytes 8388608 | tf_op jit(solution)/shard_map/slice | solution.py:26
  103.1 14.5 %all-gather.7.cloned.1.call-done = bf16[4,128,2048]{2,1,0:T(8,128)(2,1)} async-done(((bf16[4,128,1024]{2,1,0:T(8,128)(2,1)}), bf16[4,128,2048]{2,1,0:T(8,128)(2,1)}) %all-gather.7.cloned.1.call-update) | async-done | bytes 2097168 | tf_op jit(solution)/shard_map/all_gather | solution.py:33
  117.6 4.6 %multiply_reduce_fusion = f32[]{:T(128)} fusion(f32[4,128,2048]{2,1,0:T(8,128)} %bitcast.37, bf16[4,128,2048]{2,1,0:T(8,128)(2,1)} %all-gather.7.cloned.1.call-done), kind=kLoop, calls=%fused_computation.4 | loop fusion | flops 3145727 | bytes 6291460 | tf_op jit(solution)/shard_map/reduce_sum | solution.py:35
  122.2 0.6 dynamic_slice.3
  122.8 27.4 %psum.7 = f32[]{:T(128)} all-reduce(f32[]{:T(128)} %multiply_reduce_fusion), channel_id=1, replica_groups=mesh['state'=2,'bond'=16] {'bond'}, use_global_device_ids=true, to_apply=%region_1.0 | all-reduce | flops 1 | bytes 8 | tf_op jit(solution)/shard_map/psum | solution.py:35
  151.5 4.7 %broadcast_multiply_fusion = f32[4,128,2048]{2,1,0:T(8,128)} fusion(f32[]{:T(128)S(6)} %mul.17, f32[768,2048]{1,0:T(8,128)} %copy-done), kind=kLoop, calls=%fused_computation.9 | loop fusion | flops 1048576 | bytes 8388612 | tf_op jit(solution)/shard_map/mul | solution.py:39
  156.2 38.9 %all-gather.11.cloned.1.call-done = bf16[2048,2,1024]{2,0,1:T(8,128)(2,1)} async-done(((bf16[128,2,1024]{2,0,1:T(8,128)(2,1)}), bf16[2048,2,1024]{2,0,1:T(8,128)(2,1)}) %all-gather.11.cloned.1.call-update) | async-done | bytes 8388624 | tf_op jit(solution)/shard_map/all_gather | solution.py:45
  195.1 33.6 %all-gather.9.cloned.1.call-done = bf16[2,2,128,2048]{3,2,1,0:T(8,128)(2,1)} async-done(((bf16[1,2,128,2048]{3,2,1,0:T(8,128)(2,1)}), bf16[2,2,128,2048]{3,2,1,0:T(8,128)(2,1)}) %all-gather.9.cloned.1.call-update) | async-done | bytes 2097168 | tf_op jit(solution)/shard_map/all_gather | solution.py:42
  228.7 6.3 %fusion.13 = bf16[2,1024,128]{1,2,0:T(8,128)(2,1)S(1)} fusion(bf16[2,2,128,2048]{3,2,1,0:T(8,128)(2,1)} %all-gather.9.cloned.1.call-done, bf16[2048,2,1024]{2,0,1:T(8,128)(2,1)} %all-gather.11.cloned.1.call-done), kind=kOutput, calls=%fused_computation.13 | convolution fusion | flops 2147745792 | bytes 11010048 | tf_op jit(solution)/shard_map/asf,ksea->kfe/dot_general | solution.py:43
  235.0 16.1 %all_to_all.30 = bf16[2,1024,128]{1,2,0:T(8,128)(2,1)S(1)} all-to-all(bf16[2,1024,128]{1,2,0:T(8,128)(2,1)S(1)} %fusion.13), channel_id=1, replica_groups=mesh['state'=2,'bond'=16] {'state'}, dimensions={0} | all-to-all | bytes 1048576 | tf_op jit(solution)/shard_map/all_to_all | solution.py:50
  251.4 8.1 %copy.23 = bf16[1,2048,128]{2,0,1:T(2,128)(2,1)S(1)} copy(bf16[1,2048,128]{2,1,0:T(8,128)(2,1)S(1)} %bitcast.41) | data formatting | bytes 1048576 | tf_op jit(solution)/shard_map/all_to_all | solution.py:50
  259.6 0.5 broadcast
  260.1 11.6 %reduce = bf16[2048,128]{1,0:T(8,128)(2,1)S(1)} reduce(bf16[2048,1,128]{2,1,0:T(2,128)(2,1)S(1)} %bitcast.40, bf16[]{:T(256)} %broadcast), dimensions={1}, to_apply=%bitcast.36.reduce_sub_computation | reduce | bytes 1048578
  271.8 19.5 %all_to_all.31 = bf16[16,2,8192]{2,1,0:T(2,128)(2,1)S(1)} all-to-all(bf16[16,2,8192]{2,1,0:T(2,128)(2,1)S(1)} %reshape.17), channel_id=1, replica_groups=mesh['state'=2,'bond'=16] {'bond'}, dimensions={0} | all-to-all | bytes 1048576 | tf_op jit(solution)/shard_map/all_to_all | solution.py:49
  291.3 0.5 reshape.18
  292.2 1.0 copy.19
  293.2 3.4 %convert_add_fusion = f32[4,128,1024]{2,1,0:T(8,128)} fusion(f32[4,128,1024]{2,1,0:T(8,128)} %reduce-scatter.2.cloned.1.call-done, bf16[4,128,1024]{2,1,0:T(8,128)(2,1)S(1)} %copy-done.1), kind=kLoop, calls=%fused_computation.10 | loop fusion | flops 1048576 | bytes 5242880 | tf_op jit(solution)/shard_map/add | solution.py:41
  (18 shorter events, 1.0 us)
Async XLA Ops:
  7.2 77.3 %all-gather.5.cloned.1.call-start = ((), (), s32[]{:S(2)}) async-start(), calls=%async_computation.3 | async-start | bytes 8912896 | tf_op jit(solution)/shard_map/all_gather | solution.py:25
  7.9 109.7 %all-gather.7.cloned.1.call-start = ((), (), s32[]{:S(2)}) async-start(), calls=%async_computation.4 | async-start | bytes 3145728 | tf_op jit(solution)/shard_map/all_gather | solution.py:33
  8.6 186.4 %all-gather.11.cloned.1.call-start = ((), (), s32[]{:S(2)}) async-start(), calls=%async_computation.7 | async-start | bytes 8912896 | tf_op jit(solution)/shard_map/all_gather | solution.py:45
  10.7 218.0 %all-gather.9.cloned.1.call-start = ((), (), s32[]{:S(2)}) async-start(), calls=%async_computation.6 | async-start | bytes 3145728 | tf_op jit(solution)/shard_map/all_gather | solution.py:42
  94.5 2.7 copy-start
  98.4 194.8 %reduce-scatter.2.cloned.1.call-start = ((), (), s32[]{:S(2)}) async-start(), calls=%async_computation.5 | async-start | bytes 6291456 | tf_op jit(solution)/shard_map/reduce_scatter | solution.py:38
  103.1 19.1 %copy-start.2 = (f32[2]{0:T(128)S(1)}, f32[2]{0:T(128)}, u32[]{:S(2)}) copy-start(f32[2]{0:T(128)} %param.11) | copy-start | bytes 28
  260.1 33.1 %copy-start.1 = (bf16[4,128,1024]{2,1,0:T(8,128)(2,1)S(1)}, bf16[4,128,1024]{2,1,0:T(8,128)(2,1)}, u32[]{:S(2)}) copy-start(bf16[4,128,1024]{2,1,0:T(8,128)(2,1)} %param.10) | copy-start | bytes 3145732
Sparse Core Ops, SparseCore 0:
  10.1 74.2 all-gather.4
  86.0 31.5 all-gather.6
  120.4 74.6 all-gather.10
  197.1 31.5 all-gather.8
  230.8 59.9 reduce-scatter.1
where the time goes:
time: 307 us; the launch traced here: 303 us
  waiting for transfers between devices  162 us (53%)
  blocking collectives  62.9 us (20%)
  other arithmetic  24.3 us (8%)
  local copies, waits for them, and re-layouts  22 us (7%)
  matrix products  16.5 us (5%)
  between operations  15.1 us (5%)
    all_gather x1, waiting for transfers between devices, shards(): lax.all_gather(intersect_left, 'bond', axis=1, tiled=True)[0]  73.7 us
    all_gather x1, waiting for transfers between devices, shards(): lax.all_gather(current_site, 'bond', axis=0, tiled=True)  38.9 us
    all_gather x1, waiting for transfers between devices, shards(): moved_all = lax.all_gather(moved, 'state', axis=0, tiled=True)  33.6 us
    psum x1, blocking collectives, shards(): lax.psum(jnp.sum(projected * whole_block.astype(jnp.float32)), 'bond')  27.4 us
    all_to_all x1, blocking collectives, shards(): lax.all_to_all(lax.all_to_all(grown.astype(jnp.bfloat16), 'state', split_...  19.5 us
    all_to_all x1, blocking collectives, shards(): lax.all_to_all(grown.astype(jnp.bfloat16), 'state', split_axis=0, concat_...  16.1 us
    all_gather x1, waiting for transfers between devices, shards(): whole_block = lax.all_gather(current_block, 'state', axis=2, tiled=True)  14.5 us
    unnamed x1, other arithmetic  11.6 us
  transfers between devices with their start and end apart: 5, of which 4 were waited for; matrix products, arithmetic and copies ran while one was open for 19% of the time, Pallas kernels for 0%

commit v1 on v0

v1 whole, which is shorter than its diff:
```python
import functools

import jax
import jax.numpy as jnp
from jax import lax
from jax.experimental import pallas as pl
from jax.experimental.pallas import tpu as pltpu
from jax.sharding import PartitionSpec as P

MESH = pl.DeviceIdType.MESH
CORES = 2
TILE = 256


def kernel(
    states, bonds, rows_y,
    env_hbm, block_hbm, site_hbm, grow_hbm, current_hbm, weight_ref,
    pen_hbm, next_hbm,
    ebuf, abuf, stored, cbuf, psend, precv, mbuf, acc, pen, nsend, nrecv, iall,
    local_sem, out_sem, e_send, e_recv, a_send, a_recv, p_send, p_recv, m_send, m_recv,
    i_send, i_recv, n_send, n_recv, c_send, c_recv, line,
):
    nc, ny = CORES, rows_y
    nz = bonds // (nc * ny)
    rows, width = ebuf.shape[1:]
    pairs = block_hbm.shape[0]
    phys = site_hbm.shape[0]
    w = block_hbm.shape[1]
    per_group = TILE // rows
    per_row = ny * nc * rows // TILE
    groups = width // TILE
    gpp = groups // states
    fwidth = abuf.shape[2] // phys
    nfb = fwidth // w
    count = states * bonds

    k = lax.axis_index("state")
    me = lax.axis_index("bond")
    c = lax.rem(me, nc)
    y = lax.rem(lax.div(me, nc), ny)
    z = lax.div(me, nc * ny)
    flat = k * bonds + me

    def slot(zz, yy, cc):
        return (zz * ny + yy) * nc + cc

    e_load = pltpu.make_async_copy(env_hbm, ebuf.at[me], local_sem.at[0])
    a_load = pltpu.make_async_copy(grow_hbm, abuf.at[me], local_sem.at[1])
    e_load.start()
    c_loads = [
        pltpu.make_async_copy(
            current_hbm.at[:, :, pl.ds(g * TILE, TILE)], cbuf.at[k * gpp + g], local_sem.at[3]
        )
        for g in range(gpp)
    ]
    for copy in c_loads:
        copy.start()
    loads = []
    for q in range(pairs):
        loads.append(pltpu.make_async_copy(block_hbm.at[q], stored.at[pl.ds(q * w, w)], local_sem.at[2]))
    for s in range(phys):
        loads.append(
            pltpu.make_async_copy(site_hbm.at[s], stored.at[pl.ds((pairs + s) * w, w)], local_sem.at[2])
        )
    for copy in loads:
        copy.start()
    a_load.start()

    barrier = pltpu.get_barrier_semaphore()

    @pl.loop(1, count)
    def _(r):
        peer = lax.rem(flat + r, count)
        pl.semaphore_signal(
            barrier, inc=1, device_id=(lax.div(peer, bonds), lax.rem(peer, bonds)), device_id_type=MESH
        )

    pl.semaphore_wait(barrier, count - 1)

    env = (ebuf, e_send, e_recv)
    site = (abuf, a_send, a_recv)

    def copy_of(what, blk, dest):
        buf, ss, rs = what
        return pltpu.make_async_remote_copy(
            src_ref=buf.at[blk], dst_ref=buf.at[blk], send_sem=ss, recv_sem=rs.at[blk],
            device_id=(k, dest), device_id_type=MESH,
        )

    def act(what, blk, dest, drain):
        copy = copy_of(what, blk, dest)
        if drain:
            copy.wait_send()
        else:
            copy.start()

    def arrive(what, blk):
        copy_of(what, blk, me).wait_recv()

    def spread(what, blk, drain):
        @pl.when(y > 0)
        def _():
            act(what, blk, slot(z, y - 1, c), drain)

        @pl.when(y < ny - 1)
        def _():
            act(what, blk, slot(z, y + 1, c), drain)

        act(what, blk, slot(z, y, 1 - c), drain)

    def column(what, i, drain=False):
        if i == 0:
            blk = slot(z, y, c)

            @pl.when(z > 0)
            def _():
                act(what, blk, slot(z - 1, y, c), drain)

            @pl.when(z < nz - 1)
            def _():
                act(what, blk, slot(z + 1, y, c), drain)

            spread(what, blk, drain)
            return
        for sign in (1, -1):
            zz = z - sign * i
            onward = z + sign

            @pl.when(jnp.logical_and(zz >= 0, zz < nz))
            def _():
                blk = slot(zz, y, c)
                if not drain:
                    arrive(what, blk)

                @pl.when(jnp.logical_and(onward >= 0, onward < nz))
                def _():
                    act(what, blk, slot(onward, y, c), drain)

                spread(what, blk, drain)

    def turn(j):
        least = jnp.minimum(z, nz - 1 - z)
        near = (j + 1) // 2
        inner = z - near if j % 2 else z + near
        far = j - least
        outer = jnp.where(z <= nz - 1 - z, z + far, z - far)
        return jnp.where(j <= 2 * least, inner, outer)

    def across(what, j, drain=False):
        zz = turn(j)
        for u in range(1, ny):
            for sign in (1, -1):
                yy = y - sign * u
                onward = y + sign

                @pl.when(jnp.logical_and(yy >= 0, yy < ny))
                def _():
                    blk = slot(zz, yy, c)
                    if not drain:
                        arrive(what, blk)

                    @pl.when(jnp.logical_and(onward >= 0, onward < ny))
                    def _():
                        act(what, blk, slot(z, onward, c), drain)

                    act(what, blk, slot(z, y, 1 - c), drain)

    def sibling(what, j):
        zz = turn(j)
        for yy in range(ny):
            arrive(what, slot(zz, yy, 1 - c))

    def p_copy(g, peer):
        return pltpu.make_async_remote_copy(
            src_ref=psend.at[g], dst_ref=precv.at[k, lax.rem(g, gpp)], send_sem=p_send,
            recv_sem=p_recv.at[k], device_id=(peer, me), device_id_type=MESH,
        )

    def m_copy(g, peer):
        return pltpu.make_async_remote_copy(
            src_ref=mbuf.at[g, :, k], dst_ref=mbuf.at[g, :, k], send_sem=m_send,
            recv_sem=m_recv.at[k], device_id=(peer, me), device_id_type=MESH,
        )

    def c_copy(zz, peer):
        part = pl.ds(zz * per_row, per_row)
        return pltpu.make_async_remote_copy(
            src_ref=cbuf.at[part], dst_ref=cbuf.at[part], send_sem=c_send, recv_sem=c_recv.at[zz],
            device_id=(peer, me), device_id_type=MESH,
        )

    def share(drain=False):
        for j in range(nz):
            zz = turn(j)

            @pl.when(lax.div(zz * per_row, gpp) == k)
            def _():
                for other in range(1, states):
                    copy = c_copy(zz, lax.rem(k + other, states))
                    if drain:
                        copy.wait_send()
                    else:
                        copy.start()

    def project(j):
        zz = turn(j)

        @pl.when(lax.div(zz * per_row, gpp) != k)
        def _():
            c_copy(zz, k).wait_recv()

        @pl.loop(0, per_row)
        def _(r):
            g = zz * per_row + r
            left = ebuf[pl.ds(g * per_group, per_group)].reshape(TILE, width)
            prod = lax.dot_general(
                stored[...], left, (((1,), (1,)), ((), ())), preferred_element_type=jnp.float32
            )
            mbuf[g, :, k] = prod[pairs * w :].astype(jnp.bfloat16).reshape(phys, w, TILE)
            whole = prod[: pairs * w]
            here = cbuf[g].reshape(pairs * w, TILE).astype(jnp.float32)
            line[...] += jnp.sum((whole * here).reshape(pairs * w // 8, 8, TILE), axis=0)
            part = whole.astype(jnp.bfloat16)
            psend[g] = part
            owner = lax.div(g, gpp)

            @pl.when(owner == k)
            def _():
                precv[k, lax.rem(g, gpp)] = part

            for other in range(1, states):
                peer = lax.rem(k + other, states)

                m_copy(g, peer).start()

                @pl.when(owner == peer)
                def _():
                    p_copy(g, peer).start()

    def grow(j):
        zz = turn(j)

        @pl.loop(0, per_row)
        def _(r):
            g = zz * per_row + r
            right = abuf[pl.ds(g * per_group, per_group)].reshape(TILE, phys * fwidth)
            total = jnp.zeros((states * w, fwidth), jnp.float32)
            for s in range(phys):
                total = total + jnp.dot(
                    mbuf[g, s].reshape(states * w, TILE),
                    right[:, s * fwidth : (s + 1) * fwidth],
                    preferred_element_type=jnp.float32,
                )
            acc[...] += total

    def overlap():
        short = jnp.sum(line[...], axis=0, keepdims=True)
        total = short[:, :128]
        for at in range(128, TILE, 128):
            total = total + short[:, at : at + 128]
        iall[flat] = total

    def i_copy(peer):
        return pltpu.make_async_remote_copy(
            src_ref=iall.at[flat], dst_ref=iall.at[flat], send_sem=i_send, recv_sem=i_recv,
            device_id=(lax.div(peer, bonds), lax.rem(peer, bonds)), device_id_type=MESH,
        )

    def tell():
        @pl.loop(1, count)
        def _(r):
            i_copy(lax.rem(flat + r, count)).start()

    pen_copies = [
        pltpu.make_async_copy(pen.at[g], pen_hbm.at[:, :, pl.ds(g * TILE, TILE)], out_sem.at[0])
        for g in range(gpp)
    ]

    def penalize():
        rest = iall.at[pl.ds(0, count - 1)]
        pltpu.make_async_remote_copy(
            src_ref=rest, dst_ref=rest, send_sem=i_send, recv_sem=i_recv,
            device_id=(k, me), device_id_type=MESH,
        ).wait_recv()
        for other in range(1, states):
            peer = lax.rem(k + other, states)
            pltpu.make_async_remote_copy(
                src_ref=precv.at[peer], dst_ref=precv.at[peer], send_sem=p_send,
                recv_sem=p_recv.at[peer], device_id=(peer, me), device_id_type=MESH,
            ).wait_recv()
        scale = 1.0 / (phys * width)
        factors = [
            weight_ref[kk] * (jnp.sum(iall[kk * bonds : (kk + 1) * bonds]) * scale)
            for kk in range(states)
        ]
        for g in range(gpp):
            value = cbuf[k * gpp + g].reshape(pairs * w, TILE).astype(jnp.float32)
            for kk in range(states):
                value = value + factors[kk] * precv[kk, g].astype(jnp.float32)
            pen[g] = value.reshape(pairs, w, TILE)
            pen_copies[g].start()

    acc[...] = jnp.zeros_like(acc)
    line[...] = jnp.zeros_like(line)
    e_load.wait()
    for i in range(2 * nz):
        if i < nz:
            column(env, i)
        if i == 0:
            for copy in c_loads:
                copy.wait()
            share()
        if i >= nz - 1 and i - (nz - 1) < nz:
            if i == nz - 1:
                a_load.wait()
            column(site, i - (nz - 1))
        if 1 <= i <= nz:
            across(env, i - 1)
            sibling(env, i - 1)
            if i == 1:
                for copy in loads:
                    copy.wait()
            project(i - 1)
            if i == nz:
                overlap()
                tell()
        if i >= nz:
            across(site, i - nz)
            sibling(site, i - nz)
            if i == nz:
                for other in range(1, states):
                    peer = lax.rem(k + other, states)
                    mine = mbuf.at[:, :, peer]
                    pltpu.make_async_remote_copy(
                        src_ref=mine, dst_ref=mine, send_sem=m_send, recv_sem=m_recv.at[peer],
                        device_id=(peer, me), device_id_type=MESH,
                    ).wait_recv()
            grow(i - nz)
            if i == min(nz + 1, 2 * nz - 1):
                penalize()

    def n_copy(kk, fb):
        return pltpu.make_async_remote_copy(
            src_ref=nsend.at[kk, fb], dst_ref=nrecv.at[me], send_sem=n_send, recv_sem=n_recv,
            device_id=(kk, k * nfb + fb), device_id_type=MESH,
        )

    def is_me(kk, fb):
        return jnp.logical_and(k == kk, me == k * nfb + fb)

    for kk in range(states):
        for fb in range(nfb):
            part = acc[kk * w : (kk + 1) * w, fb * w : (fb + 1) * w].T.astype(jnp.bfloat16)
            nsend[kk, fb] = part

            @pl.when(is_me(kk, fb))
            def _():
                nrecv[me] = part

            @pl.when(jnp.logical_not(is_me(kk, fb)))
            def _():
                n_copy(kk, fb).start()

    inside = lax.div(me, nfb) == k

    def all_of(number):
        rest = nrecv.at[pl.ds(0, number)]
        return pltpu.make_async_remote_copy(
            src_ref=rest, dst_ref=rest, send_sem=n_send, recv_sem=n_recv,
            device_id=(k, me), device_id_type=MESH,
        )

    for i in range(nz):
        for what in (env, site):
            column(what, i, drain=True)
            across(what, i, drain=True)

    share(drain=True)

    @pl.loop(0, groups)
    def _(g):
        for other in range(1, states):
            peer = lax.rem(k + other, states)

            @pl.when(lax.div(g, gpp) == peer)
            def _():
                p_copy(g, peer).wait_send()

            m_copy(g, peer).wait_send()

    @pl.loop(1, count)
    def _(r):
        i_copy(lax.rem(flat + r, count)).wait_send()

    for copy in pen_copies:
        copy.wait()
    for kk in range(states):
        for fb in range(nfb):
            @pl.when(jnp.logical_not(is_me(kk, fb)))
            def _():
                n_copy(kk, fb).wait_send()

    @pl.when(inside)
    def _():
        all_of(bonds - 1).wait_recv()

    @pl.when(jnp.logical_not(inside))
    def _():
        all_of(bonds).wait_recv()

    store = pltpu.make_async_copy(nrecv, next_hbm, out_sem.at[1])
    store.start()
    store.wait()


def shards(states, bonds, intersect_left, stored_block, stored_site, current_site, current_block, penalty_weight):
    rows, width = intersect_left.shape[1:]
    pairs, w = stored_block.shape[1:3]
    phys = stored_site.shape[1]
    fwidth = current_site.shape[2]
    groups = width // TILE
    gpp = groups // states
    rows_y = 1
    while 4 * rows_y * rows_y <= bonds // CORES:
        rows_y *= 2
    bf, f32 = jnp.bfloat16, jnp.float32
    anywhere = pl.BlockSpec(memory_space=pl.ANY)
    dma = pltpu.SemaphoreType.DMA
    penalized, grown = pl.pallas_call(
        functools.partial(kernel, states, bonds, rows_y),
        out_shape=(
            jax.ShapeDtypeStruct(current_block.shape, f32),
            jax.ShapeDtypeStruct((bonds, w, w), bf),
        ),
        in_specs=[anywhere] * 5 + [pl.BlockSpec(memory_space=pltpu.SMEM)],
        out_specs=(anywhere, anywhere),
        scratch_shapes=[
            pltpu.VMEM((bonds, rows, width), bf),
            pltpu.VMEM((bonds, rows, phys * fwidth), bf),
            pltpu.VMEM(((pairs + phys) * w, width), bf),
            pltpu.VMEM((groups, pairs, w, TILE), bf),
            pltpu.VMEM((groups, pairs * w, TILE), bf),
            pltpu.VMEM((states, gpp, pairs * w, TILE), bf),
            pltpu.VMEM((groups, phys, states, w, TILE), bf),
            pltpu.VMEM((states * w, fwidth), f32),
            pltpu.VMEM((gpp, pairs, w, TILE), f32),
            pltpu.VMEM((states, fwidth // w, w, w), bf),
            pltpu.VMEM((bonds, w, w), bf),
            pltpu.VMEM((states * bonds, 1, 128), f32),
            dma((4,)), dma((2,)),
            dma, dma((bonds,)), dma, dma((bonds,)),
            dma, dma((states,)), dma, dma((states,)),
            dma, dma, dma, dma,
            dma, dma((bonds,)),
            pltpu.VMEM((8, TILE), f32),
        ],
        compiler_params=pltpu.CompilerParams(
            collective_id=0, has_side_effects=True, vmem_limit_bytes=60 * 1024 * 1024
        ),
    )(
        intersect_left[0], stored_block[0], stored_site[0],
        current_site.reshape(rows, phys * fwidth), current_block, penalty_weight,
    )
    return penalized, grown.transpose(1, 0, 2).reshape(1, w, bonds * w)


def solution(mesh):
    placed = (
        P("state", "bond", None),
        P("state", None, "bond", None),
        P("state", None, "bond", None),
        P("bond", None, "state"),
        P(None, "bond", "state"),
        P(),
    )
    return jax.shard_map(
        functools.partial(shards, mesh.shape["state"], mesh.shape["bond"]),
        mesh=mesh,
        in_specs=placed,
        out_specs=(P(None, "bond", "state"), P("state", "bond", None)),
        check_vma=False,
    )
```

time: 307 us -> 134 us (0.44); the launches traced: 303 us -> 134 us
  waiting for transfers between devices: 162 us -> 0 us
  Pallas kernels: 0 us -> 127 us
  blocking collectives: 62.9 us -> 0 us
  other arithmetic: 24.3 us -> 0 us
  matrix products: 16.5 us -> 0 us
  local copies, waits for them, and re-layouts: 22 us -> 5.75 us
  between operations: 15.1 us -> 0.65 us
    all_gather x4 -> x0, waiting for transfers between devices: 161 us -> none  [the longest x1 73.7 us: shards(): lax.all_gather(intersect_left, 'bond', axis=1, tiled=True)[0]]
    pallas_call x0 -> x1, Pallas kernels: none -> 127 us  [shards(): pl.pallas_call(functools.partial(kernel, states, bonds, rows_y), out_shap...]
    all_to_all x2 -> x0, blocking collectives: 35.5 us -> none  [the longest x1 19.5 us: shards(): lax.all_to_all(lax.all_to_all(grown.astype(jnp.bfloat16), 'state', split_...]
    psum x1 -> x0, blocking collectives: 27.4 us -> none  [shards(): lax.psum(jnp.sum(projected * whole_block.astype(jnp.float32)), 'bond')]
    dot_general x2 -> x0, matrix products: 16.5 us -> none  [the longest x1 10.1 us: contract_last(): lax.dot_general(left, right, (((1,), (1,)), ((), ())), preferred_element_...]
    unnamed x1 -> x0, other arithmetic: 11.6 us -> none
    all_to_all x3 -> x0, local copies, waits for them, and re-layouts: 8.69 us -> none  [the longest x2 8.41 us: shards(): lax.all_to_all(grown.astype(jnp.bfloat16), 'state', split_axis=0, concat_...]
    slice x2 -> x0, local copies, waits for them, and re-layouts: 5.78 us -> none  [the longest x1 4.66 us: shards(): products[:pair_count * column_count]]
  transfers between devices with their start and end apart: 5 -> 0, of which waited for: 4 -> 0; matrix products, arithmetic and copies ran while one was open for 19% -> 0% of each run, Pallas kernels for 0% -> 0%
where the time goes in v1:
time: 134 us
  Pallas kernels  127 us (95%)
  local copies, waits for them, and re-layouts  5.75 us (4%)
    pallas_call x1, Pallas kernels, shards(): pl.pallas_call(functools.partial(kernel, states, bonds, rows_y), out_shap...  127 us
    unnamed x5, local copies, waits for them, and re-layouts  4.29 us

profile of v1, /device:TPU:27, one launch (start us, length us, event | category | flops | bytes accessed | tf_op | source)
XLA Modules:
  0.0 133.6 jit_solution(3042384249193851340)
XLA Ops:
  0.6 2.0 %copy.10 = bf16[16,8,2,1024]{3,1,2,0:T(8,128)(2,1)} copy(bf16[16,8,2,1024]{3,2,1,0:T(2,128)(2,1)} %bitcast.11) | data formatting | bytes 1048576
  2.6 127.2 %shard_map.77 = (f32[4,128,1024]{2,1,0:T(8,128)}, bf16[16,128,128]{2,1,0:T(8,128)(2,1)}) custom-call(bf16[128,2048]{1,0:T(8,128)(2,1)} %bitcast.13, bf16[4,128,2048]{2,1,0:T(8,128)(2,1)} %bitcast.7, bf16[2,128,2048]{2,1,0:T(8,128)(2,1)} %bitcast.10, bf16[128,2048]{1,0:T(8,128)(2,1)} %bitcast.9, bf16[4,128,1024]{2,1,0:T(8,128)(2,1)} %current_hbm.1, f32[2]{0:T(128)} %weight_ref.1), custom_call_target="tpu_custom_call" | custom-call | tf_op jit(solution)/shard_map/pallas_call | solution.py:429
  129.8 0.0 copy-start
  129.8 1.5 %copy.8 = bf16[128,16,128]{0,2,1:T(8,128)(2,1)S(1)} copy(bf16[128,16,128]{2,0,1:T(8,128)(2,1)} %bitcast.12) | data formatting | bytes 1048576 | tf_op jit(solution)/shard_map/transpose | solution.py:464
  131.3 1.0 copy.9
  132.3 0.0 copy-done
  132.3 1.3 copy.12
Async XLA Ops:
  129.8 2.5 %copy-start = (f32[4,128,1024]{2,1,0:T(8,128)S(1)}, f32[4,128,1024]{2,1,0:T(8,128)}, u32[]{:S(2)}) copy-start(f32[4,128,1024]{2,1,0:T(8,128)} %get-tuple-element.10) | copy-start | bytes 6291460

commit v2 on v1

--- a/solution.py
+++ b/solution.py
@@ -97,12 +97,17 @@
     def arrive(what, blk):
         copy_of(what, blk, me).wait_recv()
 
-    def spread(what, blk, drain):
-        @pl.when(y > 0)
+    detoured = ny == 2 and nz > 2
+
+    def is_end(zz):
+        return jnp.logical_or(zz == 0, zz == nz - 1)
+
+    def spread(what, blk, drain, wide=True):
+        @pl.when(jnp.logical_and(y > 0, wide))
         def _():
             act(what, blk, slot(z, y - 1, c), drain)
 
-        @pl.when(y < ny - 1)
+        @pl.when(jnp.logical_and(y < ny - 1, wide))
         def _():
             act(what, blk, slot(z, y + 1, c), drain)
 
@@ -120,7 +125,8 @@
             def _():
                 act(what, blk, slot(z + 1, y, c), drain)
 
-            spread(what, blk, drain)
+            if not (detoured and what is site):
+                spread(what, blk, drain)
             return
         for sign in (1, -1):
             zz = z - sign * i
@@ -136,7 +142,39 @@
                 def _():
                     act(what, blk, slot(onward, y, c), drain)
 
-                spread(what, blk, drain)
+                wide = jnp.logical_not(is_end(zz)) if detoured and what is site else True
+                spread(what, blk, drain, wide)
+
+    def detour(what, d, drain=False):
+        if d == 0:
+            blk = slot(z, 1 - y, c)
+            if not drain:
+                arrive(what, blk)
+
+            @pl.when(z == 0)
+            def _():
+                act(what, blk, slot(1, y, c), drain)
+
+            @pl.when(z == nz - 1)
+            def _():
+                act(what, blk, slot(nz - 2, y, c), drain)
+
+            act(what, blk, slot(z, y, 1 - c), drain)
+            return
+        for sign, end in ((1, 0), (-1, nz - 1)):
+            onward = z + sign
+
+            @pl.when(z - sign * d == end)
+            def _():
+                blk = slot(end, 1 - y, c)
+                if not drain:
+                    arrive(what, blk)
+
+                @pl.when(jnp.logical_and(onward >= 0, onward < nz))
+                def _():
+                    act(what, blk, slot(onward, y, c), drain)
+
+                act(what, blk, slot(z, y, 1 - c), drain)
 
     def turn(j):
         least = jnp.minimum(z, nz - 1 - z)
@@ -147,13 +185,16 @@
         return jnp.where(j <= 2 * least, inner, outer)
 
     def across(what, j, drain=False):
+        if detoured and what is site and j == 0:
+            return
         zz = turn(j)
+        straight = jnp.logical_not(is_end(zz)) if detoured and what is site else True
         for u in range(1, ny):
             for sign in (1, -1):
                 yy = y - sign * u
                 onward = y + sign
 
-                @pl.when(jnp.logical_and(yy >= 0, yy < ny))
+                @pl.when(jnp.logical_and(jnp.logical_and(yy >= 0, yy < ny), straight))
                 def _():
                     blk = slot(zz, yy, c)
                     if not drain:
@@ -310,10 +351,15 @@
             for copy in c_loads:
                 copy.wait()
             share()
+            if detoured:
+                a_load.wait()
+                spread(site, me, False)
         if i >= nz - 1 and i - (nz - 1) < nz:
-            if i == nz - 1:
+            if i == nz - 1 and not detoured:
                 a_load.wait()
             column(site, i - (nz - 1))
+            if i == nz - 1 and detoured:
+                detour(site, 0)
         if 1 <= i <= nz:
             across(env, i - 1)
             sibling(env, i - 1)
@@ -326,6 +372,8 @@
                 tell()
         if i >= nz:
             across(site, i - nz)
+            if detoured and i > nz:
+                detour(site, i - nz)
             sibling(site, i - nz)
             if i == nz:
                 for other in range(1, states):
@@ -374,6 +422,10 @@
         for what in (env, site):
             column(what, i, drain=True)
             across(what, i, drain=True)
+        if detoured:
+            detour(site, i, drain=True)
+            if i == 0:
+                spread(site, me, True)
 
     share(drain=True)
 

time: 134 us -> 136 us (1.015)
  no operation moved by 1% of the time
where the time goes in v2:
time: 136 us; the launch traced here: 134 us
  Pallas kernels  128 us (94%)
  local copies, waits for them, and re-layouts  5.75 us (4%)
    pallas_call x1, Pallas kernels, shards(): pl.pallas_call(functools.partial(kernel, states, bonds, rows_y), out_shap...  128 us
    unnamed x5, local copies, waits for them, and re-layouts  4.29 us

profile of v2, /device:TPU:27, one launch (start us, length us, event | category | flops | bytes accessed | tf_op | source)
XLA Modules:
  0.0 134.4 jit_solution(12358436754504473501)
XLA Ops:
  0.6 2.0 %copy.10 = bf16[16,8,2,1024]{3,1,2,0:T(8,128)(2,1)} copy(bf16[16,8,2,1024]{3,2,1,0:T(2,128)(2,1)} %bitcast.11) | data formatting | bytes 1048576
  2.6 128.0 %shard_map.77 = (f32[4,128,1024]{2,1,0:T(8,128)}, bf16[16,128,128]{2,1,0:T(8,128)(2,1)}) custom-call(bf16[128,2048]{1,0:T(8,128)(2,1)} %bitcast.13, bf16[4,128,2048]{2,1,0:T(8,128)(2,1)} %bitcast.7, bf16[2,128,2048]{2,1,0:T(8,128)(2,1)} %bitcast.10, bf16[128,2048]{1,0:T(8,128)(2,1)} %bitcast.9, bf16[4,128,1024]{2,1,0:T(8,128)(2,1)} %current_hbm.1, f32[2]{0:T(128)} %weight_ref.1), custom_call_target="tpu_custom_call" | custom-call | tf_op jit(solution)/shard_map/pallas_call | solution.py:481
  130.6 0.0 copy-start
  130.6 1.5 %copy.8 = bf16[128,16,128]{0,2,1:T(8,128)(2,1)S(1)} copy(bf16[128,16,128]{2,0,1:T(8,128)(2,1)} %bitcast.12) | data formatting | bytes 1048576 | tf_op jit(solution)/shard_map/transpose | solution.py:516
  132.1 1.0 copy.9
  133.1 0.0 copy-done
  133.1 1.3 copy.12
Async XLA Ops:
  130.6 2.5 %copy-start = (f32[4,128,1024]{2,1,0:T(8,128)S(1)}, f32[4,128,1024]{2,1,0:T(8,128)}, u32[]{:S(2)}) copy-start(f32[4,128,1024]{2,1,0:T(8,128)} %get-tuple-element.10) | copy-start | bytes 6291460
